TPU v7x, 256 devices: a whole 4x4x8 slice. The times are simulated.
256 devices in a mesh: grp: 4 (over x), wide: 64 (over y, z, core).
Axes of the slice: x: 4, y: 4, z: 8, core: 2. Of those that a mesh axis runs over, the one named last changes fastest.
Arguments:
- leaf_entries: float32 [4, 128, 512, 512], P('grp', 'wide'), may hold values from -8 to 14, as said below
- leaf_tiles: int32 [4, 128], P('grp', 'wide'), may hold values from 1 to 3
- leaf_map: int32 [4, 128, 3], P('grp', 'wide'), may hold values from 0 to 7, as said below
- mid_entries: float32 [4, 64, 1024, 1024], P('grp', 'wide'), may hold values from -8 to 14, as said below
- mid_tiles: int32 [4, 64], P('grp', 'wide'), may hold values from 3 to 7, as said below
- mid_map: int32 [4, 64, 7], P('grp', 'wide'), may hold values from 0 to 55, as said below
- root_panel_entries: float32 [4, 7680, 512], P('grp', 'wide'), may hold values from -8 to 14, as said below
- root_update_entries: float32 [4, 64, 896, 896], P('grp', 'wide'), may hold values from -1 to 5, as said below
Outputs:
- root_panel: float32 [4, 7680, 512], P('grp', 'wide')
- top_update: float32 [64, 896, 896], P('wide', 'grp')
Inputs may be any that keep to these rules, and one draw needn't show every extreme that they name: `mid_tiles`: each group has a middle front with 7 live update tiles. `leaf_map`: the 3 entries of one leaf are distinct and less than 1 + mid_tiles of its middle front. `mid_map`: entry a of a middle front lies in the block (s + a) mod 8 of 7 consecutive tiles, s a multiple of 1 chosen for each front; so the live tiles of one middle update that land in one block of step four number at most 1, and in every draw some middle update sends exactly 1 to one block. `leaf_entries`: each leaf front is symmetric positive definite. `mid_entries`: each middle front is symmetric positive definite. `root_panel_entries`: the first 512 rows form a symmetric positive definite block. `root_update_entries`: the assembled square of step four before the additions is symmetric.
All inputs are finite; a program needn't handle non-finite values.
Results may differ from a plain program's by a relative error of at most 0.0003.
Values sent between devices are 32-bit elements; how exact they have to be, the bound alone decides.
A program may use at most 128 MiB of HBM per device.

v0:
```python
import math

import jax
import jax.numpy as jnp
from jax import lax
from jax.sharding import PartitionSpec as P

TILE = 128
UL = 3
UM = 7
FM = 8
K = 4
UT = 56
R = 60


def side_by_side(arrays, axis, split_dim, concat_dim, along):
    widths = [math.prod(a.shape[along:]) for a in arrays]
    both = jnp.concatenate(
        [a.reshape(*a.shape[:along], w) for a, w in zip(arrays, widths)], axis=along
    )
    filled = lax.all_to_all(both, axis, split_axis=split_dim, concat_axis=concat_dim, tiled=True)
    tiles = jnp.split(filled, [sum(widths[:k]) for k in range(1, len(widths))], axis=along)
    return tuple(
        (b.reshape(*filled.shape[:along], *a.shape[along:]) for a, b in zip(arrays, tiles))
    )


def factor_parts(front_mat, live_tiles):
    order_rows = front_mat.shape[0]
    tile_index = jnp.arange(order_rows, dtype=jnp.int32) // TILE
    live_rows = (tile_index < 1 + live_tiles).astype(jnp.float32)
    masked = front_mat * live_rows[:, None] * live_rows[None, :]
    pivot_factor = jnp.linalg.cholesky(masked[:TILE, :TILE])
    coupling = jax.scipy.linalg.solve_triangular(pivot_factor, masked[TILE:, :TILE].T, lower=True).T
    return (masked[TILE:, TILE:], coupling)


def partial_factor(front_mat, live_tiles):
    trail_part, coupling = factor_parts(front_mat, live_tiles)
    product = jnp.dot(
        coupling, coupling.T, precision=lax.Precision.HIGHEST, preferred_element_type=jnp.float32
    )
    return trail_part - product


def middle_assembled(leaf_fronts, leaf_live, leaf_maps, middle_front):
    leaf_updates = jax.vmap(partial_factor)(leaf_fronts, leaf_live)
    leaf_count = leaf_updates.shape[0]
    leaf_blocks = leaf_updates.reshape(leaf_count, UL, TILE, UL, TILE)
    onehot = (leaf_maps[:, None, :] == jnp.arange(FM, dtype=jnp.int32)[None, :, None]).astype(
        jnp.float32
    )
    spread = jnp.einsum("lpa,laxby->lpxby", onehot, leaf_blocks, precision=lax.Precision.HIGHEST)
    added = jnp.einsum("lpxby,lqb->pxqy", spread, onehot, precision=lax.Precision.HIGHEST)
    return middle_front + added.reshape(FM * TILE, FM * TILE)


def shards(
    leaf_entries,
    leaf_tiles,
    leaf_map,
    mid_entries,
    mid_tiles,
    mid_map,
    root_panel_entries,
    root_update_entries,
):
    devices = lax.axis_size("wide")
    position = lax.axis_index("wide")
    grid_cols = devices // 8
    row_tiles = UT // 8
    column_tiles = UT // grid_cols
    slot_count = min(UM, 8 // grid_cols)
    slot_total = devices * slot_count
    grid_row = position // grid_cols
    grid_column = position % grid_cols
    assembled = middle_assembled(leaf_entries[0], leaf_tiles[0], leaf_map[0], mid_entries[0, 0])
    targets = mid_map[0, 0]
    live_count = mid_tiles[0, 0]
    index_range = jnp.arange(UM, dtype=jnp.int32)
    live_pair = ((index_range[:, None] < live_count) & (index_range[None, :] < live_count)).reshape(
        -1
    )
    target_row = targets // row_tiles
    target_column = targets // column_tiles
    destination = (target_row[:, None] * grid_cols + target_column[None, :]).reshape(-1)
    local_spot = (
        (targets - target_row * row_tiles)[:, None] * column_tiles
        + (targets - target_column * column_tiles)[None, :]
    ).reshape(-1)
    order_index = jnp.arange(UM * UM, dtype=jnp.int32)
    earlier = (
        (destination[None, :] == destination[:, None])
        & live_pair[None, :]
        & (order_index[None, :] < order_index[:, None])
    )
    slot_rank = jnp.sum(earlier.astype(jnp.int32), axis=1)
    slot_id = destination * slot_count + slot_rank
    slot_range = jnp.arange(slot_total, dtype=jnp.int32)
    selector = ((slot_range[:, None] == slot_id[None, :]) & live_pair[None, :]).astype(jnp.float32)
    pair_select = selector.reshape(slot_total, UM, UM)
    spot_values = jnp.dot(
        selector,
        local_spot.astype(jnp.float32),
        precision=lax.Precision.HIGHEST,
        preferred_element_type=jnp.float32,
    )
    middle = partial_factor(assembled, live_count)
    outgoing = jnp.einsum(
        "sab,axby->sxy",
        pair_select,
        middle.reshape(UM, TILE, UM, TILE),
        precision=lax.Precision.HIGHEST,
    )
    received, placed = side_by_side(
        (
            outgoing.reshape(devices, slot_count, TILE, TILE),
            spot_values.reshape(devices, slot_count),
        ),
        "wide",
        0,
        0,
        2,
    )
    incoming = received.reshape(slot_total, TILE, TILE)
    spot_list = placed.reshape(slot_total)
    block_spots = jnp.arange(row_tiles * column_tiles, dtype=jnp.int32).astype(jnp.float32)
    scatter_table = (
        (block_spots[:, None] == spot_list[None, :])
        .astype(jnp.float32)
        .reshape(row_tiles, column_tiles, slot_total)
    )
    added = jnp.einsum("ijs,sxy->ixjy", scatter_table, incoming, precision=lax.Precision.HIGHEST)
    update_block = root_update_entries[0, 0] + added.reshape(row_tiles * TILE, column_tiles * TILE)
    panel = root_panel_entries[0]
    rows_here = panel.shape[0]
    all_tile = jnp.arange(R * TILE, dtype=jnp.int32) // TILE
    row_start = K * TILE + grid_row * row_tiles * TILE
    column_start = K * TILE + grid_column * column_tiles * TILE
    columns = []
    for pivot in range(K):
        column = panel[:, pivot * TILE : (pivot + 1) * TILE]
        raw_column = lax.all_gather(column, "wide", axis=0, tiled=True)
        factor = jnp.linalg.cholesky(raw_column[pivot * TILE : (pivot + 1) * TILE])
        all_rows = jax.scipy.linalg.solve_triangular(factor, raw_column.T, lower=True).T
        all_rows = jnp.where(all_tile[:, None] > pivot, all_rows, 0.0)
        whole = all_rows.at[pivot * TILE : (pivot + 1) * TILE].set(factor)
        solved = lax.dynamic_slice_in_dim(whole, position * rows_here, rows_here, 0)
        leading = jnp.where(all_tile[: K * TILE, None] > pivot, whole[: K * TILE], 0.0)
        panel = panel - jnp.dot(
            solved, leading.T, precision=lax.Precision.HIGHEST, preferred_element_type=jnp.float32
        )
        columns.append(solved)
        row_part = lax.dynamic_slice_in_dim(whole, row_start, row_tiles * TILE, 0)
        column_part = lax.dynamic_slice_in_dim(whole, column_start, column_tiles * TILE, 0)
        update_block = update_block - jnp.dot(
            row_part,
            column_part.T,
            precision=lax.Precision.HIGHEST,
            preferred_element_type=jnp.float32,
        )
    root_panel = jnp.concatenate(columns, axis=1)[None]
    top_part = lax.psum_scatter(update_block, "grp", scatter_dimension=0, tiled=True)
    return (root_panel, top_part[None])


def solution(mesh):
    placed = (
        P("grp", "wide", None, None),
        P("grp", "wide"),
        P("grp", "wide", None),
        P("grp", "wide", None, None),
        P("grp", "wide"),
        P("grp", "wide", None),
        P("grp", "wide", None),
        P("grp", "wide", None, None),
    )
    return jax.shard_map(
        shards,
        mesh=mesh,
        in_specs=placed,
        out_specs=(P("grp", "wide", None), P("wide", "grp", None)),
        check_vma=False,
    )
```

profile of v0, /device:TPU:1, one launch (start us, length us, event | category | flops | bytes accessed | tf_op | source)
XLA Modules:
  0.0 582.6 jit_solution(1309776919651574032)
XLA Ops:
  8.8 85.5 %all-gather.5.cloned.1.call-done = f32[7680,128]{1,0:T(8,128)} async-done(((f32[120,128]{1,0:T(8,128)}), f32[7680,128]{1,0:T(8,128)}) %all-gather.5.cloned.1.call-update) | async-done | bytes 3932176 | tf_op jit(solution)/shard_map/all_gather | solution.py:144
  96.1 11.7 %cholesky.125 = f32[128,128]{1,0:T(8,128)S(1)} custom-call(f32[128,128]{1,0:T(8,128)S(1)} %fusion.57), custom_call_target="Cholesky" | custom-call | tf_op jit(solution)/shard_map/jit(cholesky)/cholesky | solution.py:145
  109.2 9.8 %custom-call.23 = f32[1,128,128]{1,2,0:T(8,128)S(1)} custom-call(f32[1,128,128]{2,1,0:T(8,128)S(1)} %get-tuple-element.72), custom_call_target="InvertDiagBlocksLowerTriangular" | custom-call | tf_op jit(solution)/shard_map/jit(_solve_triangular)/triangular_solve | solution.py:146
  119.1 6.1 %fusion = f32[7680,128]{0,1:T(8,128)S(1)} fusion(f32[7680,128]{1,0:T(8,128)} %all-gather.5.cloned.1.call-done, pred[7680]{0:T(1024)(128)(4,1)S(1)} %broadcast_compare_fusion.2, f32[1,128,128]{1,2,0:T(8,128)S(1)} %custom-call.23), kind=kOutput, calls=%fused_computation.5 | convolution fusion | flops 1510932480 | bytes 7937536 | tf_op jit(solution)/shard_map/jit(_solve_triangular)/triangular_solve | solution.py:146
  125.3 1.8 copy-done.5
  129.9 1.9 copy.134
  131.9 72.4 %all-gather.7.cloned.1.call-done = f32[7680,128]{1,0:T(8,128)} async-done(((f32[120,128]{1,0:T(8,128)}), f32[7680,128]{1,0:T(8,128)}) %all-gather.7.cloned.1.call-update) | async-done | bytes 3932176 | tf_op jit(solution)/shard_map/all_gather | solution.py:144
  206.2 11.7 %cholesky.136 = f32[128,128]{1,0:T(8,128)S(1)} custom-call(f32[128,128]{1,0:T(8,128)S(1)} %fusion.55), custom_call_target="Cholesky" | custom-call | tf_op jit(solution)/shard_map/jit(cholesky)/cholesky | solution.py:145
  219.2 9.8 %custom-call.24 = f32[1,128,128]{1,2,0:T(8,128)S(1)} custom-call(f32[1,128,128]{2,1,0:T(8,128)S(1)} %get-tuple-element.70), custom_call_target="InvertDiagBlocksLowerTriangular" | custom-call | tf_op jit(solution)/shard_map/jit(_solve_triangular)/triangular_solve | solution.py:146
  229.1 6.0 %fusion.1 = f32[7680,128]{0,1:T(8,128)S(1)} fusion(f32[7680,128]{1,0:T(8,128)} %all-gather.7.cloned.1.call-done, pred[7680]{0:T(1024)(128)(4,1)S(1)} %broadcast_compare_fusion.3, f32[1,128,128]{1,2,0:T(8,128)S(1)} %custom-call.24), kind=kOutput, calls=%fused_computation.6 | convolution fusion | flops 1510932480 | bytes 7937536 | tf_op jit(solution)/shard_map/jit(_solve_triangular)/triangular_solve | solution.py:146
  235.3 1.8 copy-done.6
  240.9 24.0 %custom-call.17 = f32[2,128,128]{2,1,0:T(8,128)S(1)} custom-call(f32[2,128,128]{2,1,0:T(8,128)S(1)} %fusion.40), custom_call_target="Cholesky" | custom-call | tf_op jit(solution)/shard_map/vmap(jit(cholesky))/cholesky | solution.py:34
  265.2 19.7 %custom-call.18 = f32[2,1,128,128]{2,3,1,0:T(8,128)S(1)} custom-call(f32[2,1,128,128]{3,2,1,0:T(8,128)S(1)} %select_bitcast_fusion), custom_call_target="InvertDiagBlocksLowerTriangular" | custom-call | tf_op jit(solution)/shard_map/vmap(jit(_solve_triangular))/triangular_solve | solution.py:35
  284.9 1.5 fusion.36
  286.4 2.4 convolution_subtract_fusion
  290.4 2.0 fusion.85
  292.4 4.2 fusion.8
  296.6 3.0 copy.181
  299.6 5.4 copy.163
  305.0 5.6 copy.133
  310.6 4.0 fusion.7
  314.6 1.9 copy-done
  317.5 11.7 %cholesky.169 = f32[128,128]{1,0:T(8,128)S(1)} custom-call(f32[128,128]{1,0:T(8,128)S(1)} %fusion.49), custom_call_target="Cholesky" | custom-call | tf_op jit(solution)/shard_map/jit(cholesky)/cholesky | solution.py:34
  330.5 9.8 %custom-call.19 = f32[1,128,128]{1,2,0:T(8,128)S(1)} custom-call(f32[1,128,128]{2,1,0:T(8,128)S(1)} %fusion.47), custom_call_target="InvertDiagBlocksLowerTriangular" | custom-call | tf_op jit(solution)/shard_map/jit(_solve_triangular)/triangular_solve | solution.py:35
  340.3 1.6 fusion.23
  341.9 4.6 slice_subtract_fusion
  346.6 2.4 reshape.474
  349.0 4.9 copy.164
  354.1 4.9 convolution_bitcast_fusion
  359.3 6.3 %copy.148 = f32[64,1,16385]{2,1,0:T(1,128)} copy(f32[64,1,16385]{2,0,1:T(8,128)S(1)} %pad_maximum_fusion) | data formatting | bytes 8389120 | tf_op jit(solution)/shard_map/concatenate | solution.py:19
  365.6 6.5 %all-to-all-start = ((f32[64,1,16385]{2,1,0:T(1,128)}), f32[64,1,16385]{2,1,0:T(1,128)}, u32[]{:S(2)}, u32[]{:S(2)}) async-start(f32[64,1,16385]{2,1,0:T(1,128)} %copy.148), calls=%async_computation | async-start | bytes 8454144 | tf_op jit(solution)/shard_map/all_to_all | solution.py:22
  374.2 11.7 %cholesky.147 = f32[128,128]{1,0:T(8,128)S(1)} custom-call(f32[128,128]{1,0:T(8,128)S(1)} %fusion.53), custom_call_target="Cholesky" | custom-call | tf_op jit(solution)/shard_map/jit(cholesky)/cholesky | solution.py:145
  387.3 9.8 %custom-call.25 = f32[1,128,128]{1,2,0:T(8,128)S(1)} custom-call(f32[1,128,128]{2,1,0:T(8,128)S(1)} %get-tuple-element.68), custom_call_target="InvertDiagBlocksLowerTriangular" | custom-call | tf_op jit(solution)/shard_map/jit(_solve_triangular)/triangular_solve | solution.py:146
  397.2 6.0 %fusion.2 = f32[7680,128]{0,1:T(8,128)S(1)} fusion(f32[7680,128]{1,0:T(8,128)} %all-gather.9.cloned.1.call-done, pred[7680]{0:T(1024)(128)(4,1)S(1)} %broadcast_compare_fusion.1, f32[1,128,128]{1,2,0:T(8,128)S(1)} %custom-call.25), kind=kOutput, calls=%fused_computation.7 | convolution fusion | flops 1510932480 | bytes 7937536 | tf_op jit(solution)/shard_map/jit(_solve_triangular)/triangular_solve | solution.py:146
  403.3 1.8 copy-done.4
  407.4 5.6 fusion.33
  413.0 60.5 %all-to-all-done = f32[64,1,16385]{2,1,0:T(1,128)} async-done(((f32[64,1,16385]{2,1,0:T(1,128)}), f32[64,1,16385]{2,1,0:T(1,128)}, u32[]{:S(2)}, u32[]{:S(2)}) %all-to-all-start) | async-done | bytes 4194592 | tf_op jit(solution)/shard_map/all_to_all | solution.py:22
  473.5 2.7 split.8
  477.5 4.7 fusion.20
  482.2 2.1 copy.150
  484.3 3.9 fusion.30
  488.2 6.0 %fusion.27 = f32[896,896]{1,0:T(8,128)} fusion(f32[7680,128]{0,1:T(8,128)} %copy-done.4, s32[]{:T(128)S(6)} %select_n.163, s32[]{:T(128)S(6)} %select_n.161), kind=kOutput, calls=%fused_computation.40 | convolution fusion | flops 1233125376 | bytes 4128776 | tf_op jit(solution)/shard_map/dot_general | solution.py:157
  496.0 11.7 %cholesky.158 = f32[128,128]{1,0:T(8,128)S(1)} custom-call(f32[128,128]{1,0:T(8,128)S(1)} %fusion.51), custom_call_target="Cholesky" | custom-call | tf_op jit(solution)/shard_map/jit(cholesky)/cholesky | solution.py:145
  509.7 11.3 %custom-call.26 = f32[1,128,128]{1,2,0:T(8,128)} custom-call(f32[1,128,128]{2,1,0:T(8,128)} %get-tuple-element.66), custom_call_target="InvertDiagBlocksLowerTriangular" | custom-call | tf_op jit(solution)/shard_map/jit(_solve_triangular)/triangular_solve | solution.py:146
  521.1 6.2 %fusion.3 = f32[7680,128]{0,1:T(8,128)S(1)} fusion(f32[7680,128]{1,0:T(8,128)} %all-gather.11.cloned.1.call-done, pred[7680]{0:T(1024)(128)(4,1)S(1)} %broadcast_compare_fusion, f32[1,128,128]{1,2,0:T(8,128)} %custom-call.26), kind=kOutput, calls=%fused_computation.8 | convolution fusion | flops 1510932480 | bytes 7937536 | tf_op jit(solution)/shard_map/jit(_solve_triangular)/triangular_solve | solution.py:146
  527.3 1.9 copy-done.7
  529.2 8.6 %fusion.18 = f32[896,896]{1,0:T(8,128)} fusion(f32[896,896]{1,0:T(8,128)} %fusion.27, f32[896,896]{1,0:T(8,128)S(1)} %fusion.30, f32[896,896]{1,0:T(8,128)S(1)} %copy-done.2, f32[112,8,7,128]{3,2,1,0:T(8,128)S(1)} %bitcast.178, f32[1,1,896,896]{3,2,1,0:T(8,128)} %param.26, f32[7680,128]{0,1:T(8,128)S(1)} %constant_dynamic-update-slice_fusion, ...), kind=kOutput, calls=%fused_computation.27 | convolution fusion | flops 1237139456 | bytes 20643848 | tf_op jit(solution)/shard_map/dot_general | solution.py:157
  539.7 36.2 %reduce-scatter.2.cloned.1.call-done = f32[224,896]{1,0:T(8,128)} async-done(((f32[896,896]{1,0:T(8,128)}), f32[224,896]{1,0:T(8,128)}) %reduce-scatter.2.cloned.1.call-update) | async-done | bytes 802832 | tf_op jit(solution)/shard_map/reduce_scatter | solution.py:164
  (122 shorter events, 31.5 us)
Async XLA Ops:
  7.2 87.1 %all-gather.5.cloned.1.call-start = ((), (), s32[]{:S(2)}) async-start(), calls=%async_computation.2 | async-start | bytes 3993600 | tf_op jit(solution)/shard_map/all_gather | solution.py:144
  8.7 195.7 %all-gather.7.cloned.1.call-start = ((), (), s32[]{:S(2)}) async-start(), calls=%async_computation.3 | async-start | bytes 3993600 | tf_op jit(solution)/shard_map/all_gather | solution.py:144
  119.1 8.0 %copy-start.9 = (f32[1,120,512]{2,1,0:T(8,128)S(1)}, f32[1,120,512]{2,1,0:T(8,128)}, u32[]{:S(2)}) copy-start(f32[1,120,512]{2,1,0:T(8,128)} %param.25) | copy-start | bytes 737284
  119.1 9.4 %copy-start.11 = (s32[1,1,7]{2,1,0:T(1,128)S(1)}, s32[1,1,7]{2,1,0:T(1,128)}, u32[]{:S(2)}) copy-start(s32[1,1,7]{2,1,0:T(1,128)} %param.24) | copy-start | bytes 88
  125.2 6.7 %copy-start.12 = (s32[1,2]{1,0:T(1,128)S(1)}, s32[1,2]{1,0:T(1,128)}, u32[]{:S(2)}) copy-start(s32[1,2]{1,0:T(1,128)} %param.20) | copy-start | bytes 28
  125.2 1.9 copy-start.5
  128.1 244.2 %all-gather.9.cloned.1.call-start = ((), (), s32[]{:S(2)}) async-start(), calls=%async_computation.4 | async-start | bytes 3993600 | tf_op jit(solution)/shard_map/all_gather | solution.py:144
  235.2 1.9 copy-start.6
  237.5 47.4 %copy-start.8 = (f32[120,512]{1,0:T(8,128)}, f32[120,512]{1,0:T(8,128)S(1)}, u32[]{:S(2)}) copy-start(f32[120,512]{1,0:T(8,128)S(1)} %convolution_subtract_fusion.1) | copy-start | bytes 737284
  238.5 1.4 copy-start.3
  286.4 4.0 copy-start.10
  314.6 1.9 copy-start
  365.6 107.9 %all-to-all-start = ((f32[64,1,16385]{2,1,0:T(1,128)}), f32[64,1,16385]{2,1,0:T(1,128)}, u32[]{:S(2)}, u32[]{:S(2)}) async-start(f32[64,1,16385]{2,1,0:T(1,128)} %copy.148), calls=%async_computation | async-start | bytes 8454144 | tf_op jit(solution)/shard_map/all_to_all | solution.py:22
  372.1 122.1 %all-gather.11.cloned.1.call-start = ((), (), s32[]{:S(2)}) async-start(), calls=%async_computation.5 | async-start | bytes 3993600 | tf_op jit(solution)/shard_map/all_gather | solution.py:144
  403.2 1.9 copy-start.4
  407.1 168.9 %reduce-scatter.2.cloned.1.call-start = ((), (), s32[]{:S(2)}) async-start(), calls=%async_computation.6 | async-start | bytes 4014080 | tf_op jit(solution)/shard_map/reduce_scatter | solution.py:164
  521.1 8.1 %copy-start.1 = (f32[7,128,7,128]{3,2,1,0:T(8,128)S(1)}, f32[7,128,7,128]{3,2,1,0:T(8,128)}, u32[]{:S(2)}) copy-start(f32[7,128,7,128]{3,2,1,0:T(8,128)} %copy.150) | copy-start | bytes 9633796
  521.1 8.1 %copy-start.2 = (f32[896,896]{1,0:T(8,128)S(1)}, f32[896,896]{1,0:T(8,128)}, u32[]{:S(2)}) copy-start(f32[896,896]{1,0:T(8,128)} %fusion.33) | copy-start | bytes 9633796
  527.3 1.9 copy-start.7
Sparse Core Ops, SparseCore 0:
  11.2 83.0 all-gather.4
  128.3 76.0 all-gather.6
  238.3 76.5 all-gather.8
  407.2 84.0 all-gather.10
  538.0 37.9 reduce-scatter.1
where the time goes:
time: 592 us; the launch traced here: 583 us
  waiting for transfers between devices  255 us (43%)
  other arithmetic  172 us (29%)
  matrix products  75.9 us (13%)
  local copies, waits for them, and re-layouts  57.1 us (10%)
  between operations  15.4 us (3%)
  starting transfers between devices  7.37 us (1%)
    all_gather x4, waiting for transfers between devices, shards(): raw_column = lax.all_gather(column, 'wide', axis=0, tiled=True)  158 us
    all_to_all x1, waiting for transfers between devices, side_by_side(): lax.all_to_all(both, axis, split_axis=split_dim, concat_axis=concat_dim,...  60.5 us
    another operation x13, other arithmetic, shards(): factor = jnp.linalg.cholesky(raw_column[pivot * TILE:(pivot + 1) * TILE])  49.6 us
    another operation x9, other arithmetic, shards(): jax.scipy.linalg.solve_triangular(factor, raw_column.T, lower=True)  44 us
    another operation x6, other arithmetic, factor_parts(): pivot_factor = jnp.linalg.cholesky(masked[:TILE, :TILE])  36.5 us
    reduce_scatter x1, waiting for transfers between devices, shards(): lax.psum_scatter(update_block, 'grp', scatter_dimension=0, tiled=True)  36.2 us
    another operation x4, other arithmetic, factor_parts(): jax.scipy.linalg.solve_triangular(pivot_factor, masked[TILE:, :TILE].T, l...  30.2 us
    another operation x4, matrix products, shards(): jax.scipy.linalg.solve_triangular(factor, raw_column.T, lower=True)  24.4 us
  transfers between devices with their start and end apart: 6, of which 4 were waited for; matrix products, arithmetic and copies ran while one was open for 32% of the time, Pallas kernels for 0%

commit v1 on v0

v1 whole, which is shorter than its diff:
```python
import functools

import jax
import jax.numpy as jnp
from jax import lax
from jax.experimental import pallas as pl
from jax.experimental.pallas import tpu as pltpu
from jax.sharding import PartitionSpec as P

TILE = 128
UL = 3
UM = 7
K = 4
UR = 7
UC = 7
BLOCK = UR * TILE
PIVOT = K * TILE
SLOT = TILE + 8
MESH = pl.DeviceIdType.MESH
HIGHEST = lax.Precision.HIGHEST
NN = ((1,), (0,))
NT = ((1,), (1,))
TN = ((0,), (0,))
VMEM_BYTES = 60 * 1024 * 1024


def dot_exact(a, b, dims=NN):
    return lax.dot_general(
        a, b, (dims, ((), ())), precision=HIGHEST, preferred_element_type=jnp.float32
    )


def split_high_low(a):
    high = a.astype(jnp.bfloat16)
    low = (a - high.astype(jnp.float32)).astype(jnp.bfloat16)
    return high, low


def dot_split(a, b):
    a_high, a_low = split_high_low(a)
    b_high, b_low = split_high_low(b)
    left = jnp.concatenate([a_high, a_high, a_low], axis=1)
    right = jnp.concatenate([b_high, b_low, b_high], axis=1)
    return lax.dot_general(left, right, (NT, ((), ())), preferred_element_type=jnp.float32)


def base_factor(mats, n):
    count = n // 8
    number = range(len(mats))
    rest = [[m[8 * i : 8 * i + 8, :] for i in range(count)] for m in mats]
    row = lax.broadcasted_iota(jnp.int32, (8, n), 0)
    col = lax.broadcasted_iota(jnp.int32, (8, n), 1)
    unit = [[(row + 8 * i == col).astype(jnp.float32) for i in range(count)] for _ in mats]
    upper = [[None] * count for _ in mats]
    inverse = [[None] * count for _ in mats]

    def spread(v, j):
        return jnp.broadcast_to(v[j : j + 1, :], (8, n))

    for kb in range(count):
        cols = [
            [
                [
                    jnp.broadcast_to(rest[p][i][:, 8 * kb + j : 8 * kb + j + 1], (8, n))
                    for i in range(kb, count)
                ]
                for j in range(8)
            ]
            for p in number
        ]
        top = [rest[p][kb] for p in number]
        top_unit = [unit[p][kb] for p in number]
        us = [[] for _ in mats]
        xs = [[] for _ in mats]
        for j in range(8):
            for p in number:
                scale = lax.rsqrt(spread(cols[p][j][0], j))
                cols[p][j] = [c * scale for c in cols[p][j]]
                us[p].append(spread(top[p], j) * scale)
                xs[p].append(spread(top_unit[p], j) * scale)
                if j < 7:
                    top[p] = top[p] - cols[p][j][0] * us[p][j]
                    top_unit[p] = top_unit[p] - cols[p][j][0] * xs[p][j]
                for later in range(j + 1, 8):
                    factor = spread(cols[p][j][0], later)
                    cols[p][later] = [c - d * factor for c, d in zip(cols[p][later], cols[p][j])]
        for p in number:
            u, x = us[p][0], xs[p][0]
            for j in range(1, 8):
                u = jnp.where(row == j, us[p][j], u)
                x = jnp.where(row == j, xs[p][j], x)
            upper[p][kb] = jnp.where(col >= row + 8 * kb, u, 0.0)
            inverse[p][kb] = x
            for i in range(kb + 1, count):
                a, b = rest[p][i], unit[p][i]
                for j in range(8):
                    a = a - cols[p][j][i - kb] * us[p][j]
                    b = b - cols[p][j][i - kb] * xs[p][j]
                rest[p][i], unit[p][i] = a, b
    return [jnp.concatenate(u, 0) for u in upper], [jnp.concatenate(x, 0) for x in inverse]


def factor_all(mats, n=TILE):
    if n == 32:
        return base_factor(mats, n)
    h = n // 2
    u1, x1 = factor_all([m[:h, :h] for m in mats], h)
    u12 = [dot_exact(x, m[:h, h:]) for x, m in zip(x1, mats)]
    below = [m[h:, h:] - dot_exact(u, u, TN) for m, u in zip(mats, u12)]
    u2, x2 = factor_all(below, h)
    mixed = [dot_exact(u, x, TN) for u, x in zip(u12, x1)]
    x21 = [-dot_exact(x, t) for x, t in zip(x2, mixed)]
    zero = jnp.zeros((h, h), jnp.float32)

    def stack(a, b, c, d):
        return jnp.concatenate(
            [jnp.concatenate([a, b], axis=1), jnp.concatenate([c, d], axis=1)], axis=0
        )

    upper = [stack(a, b, zero, d) for a, b, d in zip(u1, u12, u2)]
    inverse = [stack(a, zero, c, d) for a, c, d in zip(x1, x21, x2)]
    return upper, inverse


def fronts_kernel(
    leaf_tiles, leaf_map, mid_tiles, mid_map, leaf_ref, mid_ref, slot_ref, whole_ref, couple_ref
):
    whole_ref[...] = mid_ref[...]
    slot_ref[...] = jnp.zeros_like(slot_ref)
    leaves = leaf_ref.shape[0]
    _, inverse = factor_all([leaf_ref[i, :TILE, :TILE] for i in range(leaves)])
    for i in range(leaves):
        live = leaf_tiles[i]
        coupling = dot_exact(leaf_ref[i, TILE:, :TILE], inverse[i], NT)
        update = leaf_ref[i, TILE:, TILE:] - dot_split(coupling, coupling)
        for a in range(UL):
            for b in range(UL):

                @pl.when((a < live) & (b < live))
                def _():
                    rows = pl.ds(pl.multiple_of(leaf_map[i * UL + a] * TILE, TILE), TILE)
                    columns = pl.ds(pl.multiple_of(leaf_map[i * UL + b] * TILE, TILE), TILE)
                    whole_ref[rows, columns] += update[
                        a * TILE : (a + 1) * TILE, b * TILE : (b + 1) * TILE
                    ]

    _, inverse = factor_all([whole_ref[:TILE, :TILE]])
    couple_ref[...] = dot_exact(whole_ref[TILE:, :TILE], inverse[0], NT)
    live = mid_tiles[0]
    column_spots = lax.broadcasted_iota(jnp.int32, (8, TILE), 1)
    for a in range(UM):
        rows = pl.ds(a * TILE, TILE)
        product = dot_split(couple_ref[rows, :], couple_ref[...])
        update = whole_ref[pl.ds((a + 1) * TILE, TILE), TILE:] - product
        target_row = mid_map[a]
        for b in range(UM):

            @pl.when((a < live) & (b < live))
            def _():
                target_column = mid_map[b]
                row_block, column_block = target_row // UR, target_column // UC
                slot = row_block * 8 + column_block
                slot_ref[slot, :TILE, :] = update[:, b * TILE : (b + 1) * TILE]
                spot = (target_row - row_block * UR) * UC + (target_column - column_block * UC)
                slot_ref[slot, TILE:, :] = jnp.broadcast_to(
                    (spot + 1).astype(jnp.float32), (8, TILE)
                )


def solve_rows(rows, lower, inverse):
    solved = []
    for k in range(K):
        part = rows[:, k * TILE : (k + 1) * TILE]
        for j in range(k):
            part = part - dot_split(solved[j], lower[k][j])
        solved.append(dot_split(part, inverse[k]))
    return solved


def root_kernel(position, pivot_ref, row_ref, column_ref, own_ref, entry_ref, panel_ref, block_ref, lower_ref, left_ref, right_ref):
    tile = lambda i, j: pivot_ref[i * TILE : (i + 1) * TILE, j * TILE : (j + 1) * TILE]
    rest = {(i, j): tile(i, j) for i in range(K) for j in range(i + 1)}
    lower = [[None] * K for _ in range(K)]
    inverse = []
    lower_ref[...] = jnp.zeros_like(lower_ref)
    for k in range(K):
        u, x = factor_all([rest[k, k]])
        inverse.append(x[0])
        lower[k][k] = u[0].T
        for i in range(k + 1, K):
            lower[i][k] = dot_exact(rest[i, k], x[0], NT)
        for i in range(k + 1, K):
            for j in range(k + 1, i + 1):
                rest[i, j] = rest[i, j] - dot_exact(lower[i][k], lower[j][k], NT)
        for i in range(k, K):
            lower_ref[i * TILE : (i + 1) * TILE, k * TILE : (k + 1) * TILE] = lower[i][k]
        columns = slice(k * TILE, (k + 1) * TILE)
        for source, target in ((row_ref, left_ref), (column_ref, right_ref)):
            part = source[:, columns]
            for j in range(k):
                part = part - dot_split(target[:, j * TILE : (j + 1) * TILE], lower[k][j])
            target[:, columns] = dot_split(part, x[0])
    own = jnp.concatenate(solve_rows(own_ref[...], lower, inverse), axis=1)
    rows_here = own_ref.shape[0]
    first = position[0] * rows_here
    start = pl.multiple_of(jnp.minimum(first, PIVOT), 8)
    index = first + lax.broadcasted_iota(jnp.int32, own.shape, 0)
    panel_ref[...] = jnp.where(index < PIVOT, lower_ref[pl.ds(start, rows_here), :], own)
    for a in range(UR):
        rows = slice(a * TILE, (a + 1) * TILE)
        block_ref[rows, :] = entry_ref[rows, :] - dot_split(left_ref[rows, :], right_ref[...])


def add_kernel(spots, base_ref, tiles_ref, out_ref):
    out_ref[...] = base_ref[...]

    def step(s, carry):
        spot = spots[s] - 1

        @pl.when(spot >= 0)
        def _():
            rows = pl.ds(pl.multiple_of((spot // UC) * TILE, TILE), TILE)
            columns = pl.ds(pl.multiple_of((spot % UC) * TILE, TILE), TILE)
            out_ref[rows, columns] += tiles_ref[s, :TILE, :]

        return carry

    lax.fori_loop(0, tiles_ref.shape[0], step, 0)


def gather_kernel(
    panel_ref,
    row_ref,
    column_ref,
    pivot_ref,
    first_send,
    local_sem,
    row_first,
    column_first,
    pivot_first,
    row_send,
    row_recv,
    column_send,
    column_recv,
    pivot_send,
    pivot_recv,
):
    group = lax.axis_index("grp")
    me = lax.axis_index("wide")
    p, q = me // 8, me % 8
    core = me % 2
    line = me // 16
    depth = (me // 2) % 8
    devices = pivot_ref.shape[0]
    here = panel_ref.shape[0]
    there = row_ref.shape[1]

    def remote(source, target, send, recv, device):
        return pltpu.make_async_remote_copy(
            src_ref=source,
            dst_ref=target,
            send_sem=send,
            recv_sem=recv,
            device_id=(group, device),
            device_id_type=MESH,
        )

    def routes(i):
        chunk = here * me + i
        is_pivot = chunk < devices
        other = jnp.maximum(chunk - devices, 0)
        piece, slot = other // there, other % there
        block, part = piece // 8, piece % 8
        is_panel = jnp.logical_not(is_pivot)
        home = jnp.minimum(chunk, devices - 1)
        return (
            (row_ref.at[part, slot], row_first.at[slot], piece, is_panel),
            (column_ref.at[part, slot], column_first.at[slot], part * 8 + block, is_panel),
            (pivot_ref.at[home], pivot_first.at[0], home, is_pivot),
        )

    def first():
        for i in range(here):
            for which, (target, sem, device, wanted) in enumerate(routes(i)):

                @pl.when(wanted & (device != me))
                def _():
                    remote(panel_ref.at[i], target, first_send.at[which, i], sem, device).start()

                @pl.when(wanted & (device == me))
                def _():
                    pltpu.make_async_copy(panel_ref.at[i], target, local_sem.at[which, i]).start()

    def arrived(target, sem, source):
        @pl.when(source != me)
        def _():
            remote(panel_ref.at[0], target, first_send.at[0, 0], sem, me).wait_recv()

    first()
    for i in range(here):
        for which, (target, sem, device, wanted) in enumerate(routes(i)):

            @pl.when(wanted & (device == me))
            def _():
                pltpu.make_async_copy(panel_ref.at[i], target, local_sem.at[which, i]).wait()

    sends = []

    def push(source, send, recv, device):
        copy = remote(source, source, send, recv, device)
        copy.start()
        sends.append(copy)

    def landed(target, send, recv):
        remote(target, target, send, recv, me).wait_recv()

    arrived(pivot_ref.at[me], pivot_first.at[0], me // here)
    partner = me + 1 - 2 * core
    push(pivot_ref.at[me], pivot_send.at[0], pivot_recv.at[0], partner)
    for slot in range(there):
        arrived(row_ref.at[q, slot], row_first.at[slot], (devices + there * me + slot) // here)
    for step in range(1, 4):
        push(row_ref.at[q], row_send.at[step], row_recv.at[q // 2], p * 8 + (q + 2 * step) % 8)
    push(row_ref.at[q], row_send.at[0], row_recv.at[4 + q // 2], partner)
    turned = q * 8 + p
    for slot in range(there):
        arrived(column_ref.at[p, slot], column_first.at[slot], (devices + there * turned + slot) // here)
    across = p + 1 - 2 * (p % 2)
    push(column_ref.at[p], column_send.at[0], column_recv.at[16], across * 8 + q)
    for step in range(1, 4):
        push(column_ref.at[p], column_send.at[step], column_recv.at[p], ((p + 2 * step) % 8) * 8 + q)
    landed(pivot_ref.at[partner], pivot_send.at[0], pivot_recv.at[0])
    pair = pivot_ref.at[pl.ds(me - core, 2)]
    for step in range(1, 8):
        push(pair, pivot_send.at[step], pivot_recv.at[1 + depth], line * 16 + ((depth + step) % 8) * 2 + core)
    landed(column_ref.at[across], column_send.at[0], column_recv.at[16])
    for step in range(1, 4):
        push(
            column_ref.at[across], column_send.at[3 + step], column_recv.at[8 + across], ((p + 2 * step) % 8) * 8 + q
        )
    for step in range(1, 4):
        source = (q + 8 - 2 * step) % 8
        landed(row_ref.at[source], row_send.at[step], row_recv.at[source // 2])
        push(row_ref.at[source], row_send.at[3 + step], row_recv.at[4 + source // 2], partner)
    for step in range(1, 8):
        source = (depth + 8 - step) % 8
        landed(pivot_ref.at[pl.ds(line * 16 + source * 2, 2)], pivot_send.at[step], pivot_recv.at[1 + source])
    mine = pivot_ref.at[pl.ds(line * 16, 16)]
    for step in range(1, 4):
        push(mine, pivot_send.at[7 + step], pivot_recv.at[9 + line], ((line + step) % 4) * 16 + depth * 2 + core)
    for step in range(4):
        source = (q + 1 - 2 * core + 2 * step) % 8
        landed(row_ref.at[source], row_send.at[0], row_recv.at[4 + source // 2])
    for step in range(1, 4):
        source = (p + 8 - 2 * step) % 8
        landed(column_ref.at[source], column_send.at[step], column_recv.at[source])
        source = (across + 8 - 2 * step) % 8
        landed(column_ref.at[source], column_send.at[3 + step], column_recv.at[8 + source])
    for step in range(1, 4):
        source = (line + 4 - step) % 4
        landed(pivot_ref.at[pl.ds(source * 16, 16)], pivot_send.at[7 + step], pivot_recv.at[9 + source])
    for copy in sends:
        copy.wait_send()
    for i in range(here):
        for which, (target, sem, device, wanted) in enumerate(routes(i)):

            @pl.when(wanted & (device != me))
            def _():
                remote(panel_ref.at[i], target, first_send.at[which, i], sem, device).wait_send()


def vmem():
    return pl.BlockSpec(memory_space=pltpu.VMEM)


def smem():
    return pl.BlockSpec(memory_space=pltpu.SMEM)


def shape(*dims):
    return jax.ShapeDtypeStruct(dims, jnp.float32)


def shards(
    leaf_entries,
    leaf_tiles,
    leaf_map,
    mid_entries,
    mid_tiles,
    mid_map,
    root_panel_entries,
    root_update_entries,
):
    devices = lax.axis_size("wide")
    position = lax.axis_index("wide").astype(jnp.int32).reshape(1)
    panel = root_panel_entries[0]
    rows_here = panel.shape[0]
    width = panel.shape[1]
    chunks = rows_here // 8
    piece = chunks - 1
    row_rows, column_rows, pivot = pl.pallas_call(
        gather_kernel,
        out_shape=[
            shape(8, piece, 8, width),
            shape(8, piece, 8, width),
            shape(devices, 8, width),
        ],
        in_specs=[pl.BlockSpec(memory_space=pl.ANY)],
        out_specs=[vmem()] * 3,
        scratch_shapes=[
            pltpu.SemaphoreType.DMA((3, chunks)),
            pltpu.SemaphoreType.DMA((3, chunks)),
            pltpu.SemaphoreType.DMA((piece,)),
            pltpu.SemaphoreType.DMA((piece,)),
            pltpu.SemaphoreType.DMA((1,)),
            pltpu.SemaphoreType.DMA((7,)),
            pltpu.SemaphoreType.DMA((8,)),
            pltpu.SemaphoreType.DMA((7,)),
            pltpu.SemaphoreType.DMA((17,)),
            pltpu.SemaphoreType.DMA((11,)),
            pltpu.SemaphoreType.DMA((13,)),
        ],
        compiler_params=pltpu.CompilerParams(has_side_effects=True),
        name="gather",
    )(panel.reshape(chunks, 8, width))
    row_rows = row_rows.reshape(BLOCK, width)
    column_rows = column_rows.reshape(BLOCK, width)
    pivot = pivot.reshape(PIVOT, width)
    slots = pl.pallas_call(
        fronts_kernel,
        out_shape=shape(devices, SLOT, TILE),
        in_specs=[smem()] * 4 + [vmem()] * 2,
        out_specs=vmem(),
        scratch_shapes=[
            pltpu.VMEM(mid_entries.shape[2:], jnp.float32),
            pltpu.VMEM((BLOCK, TILE), jnp.float32),
        ],
        compiler_params=pltpu.CompilerParams(vmem_limit_bytes=VMEM_BYTES),
        cost_estimate=pl.CostEstimate(flops=20_000_000_000, bytes_accessed=11_000_000, transcendentals=0),
        name="fronts",
    )(
        leaf_tiles[0],
        leaf_map[0].reshape(-1),
        mid_tiles[0],
        mid_map[0, 0],
        leaf_entries[0],
        mid_entries[0, 0],
    )
    received = lax.all_to_all(slots, "wide", split_axis=0, concat_axis=0, tiled=True)
    root_panel, block = pl.pallas_call(
        root_kernel,
        out_shape=[shape(rows_here, width), shape(BLOCK, BLOCK)],
        in_specs=[smem()] + [vmem()] * 5,
        out_specs=[vmem()] * 2,
        scratch_shapes=[
            pltpu.VMEM((PIVOT + rows_here, PIVOT), jnp.float32),
            pltpu.VMEM((BLOCK, PIVOT), jnp.float32),
            pltpu.VMEM((BLOCK, PIVOT), jnp.float32),
        ],
        compiler_params=pltpu.CompilerParams(vmem_limit_bytes=VMEM_BYTES),
        cost_estimate=pl.CostEstimate(flops=30_000_000_000, bytes_accessed=11_000_000, transcendentals=0),
        name="root",
    )(position, pivot, row_rows, column_rows, panel, root_update_entries[0, 0])
    spots = received[:, TILE, 0].astype(jnp.int32)
    total = pl.pallas_call(
        add_kernel,
        out_shape=shape(BLOCK, BLOCK),
        in_specs=[smem(), vmem(), vmem()],
        out_specs=vmem(),
        compiler_params=pltpu.CompilerParams(vmem_limit_bytes=VMEM_BYTES),
        name="add_tiles",
    )(spots, block, received)
    top_part = lax.psum_scatter(total, "grp", scatter_dimension=0, tiled=True)
    return (root_panel[None], top_part[None])


def solution(mesh):
    placed = (
        P("grp", "wide", None, None),
        P("grp", "wide"),
        P("grp", "wide", None),
        P("grp", "wide", None, None),
        P("grp", "wide"),
        P("grp", "wide", None),
        P("grp", "wide", None),
        P("grp", "wide", None, None),
    )
    return jax.shard_map(
        shards,
        mesh=mesh,
        in_specs=placed,
        out_specs=(P("grp", "wide", None), P("wide", "grp", None)),
        check_vma=False,
    )
```

time: 592 us -> 310 us (0.52); the launches traced: 583 us -> 310 us
  Pallas kernels: 0 us -> 239 us
  waiting for transfers between devices: 255 us -> 38.9 us
  other arithmetic: 172 us -> 2.69 us
  matrix products: 75.9 us -> 0 us
  local copies, waits for them, and re-layouts: 57.1 us -> 1.27 us
    pallas_call x0 -> x4, Pallas kernels: none -> 239 us  [the longest x1 175 us: shards(): pl.pallas_call(gather_kernel, out_shape=[shape(8, piece, 8, width), shape...]
    another operation x32 -> x0, other arithmetic: 160 us -> none  [the longest x13 49.6 us: shards(): factor = jnp.linalg.cholesky(raw_column[pivot * TILE:(pivot + 1) * TILE])]
    all_gather x4 -> x0, waiting for transfers between devices: 158 us -> none  [shards(): raw_column = lax.all_gather(column, 'wide', axis=0, tiled=True)]
    all_to_all x1, waiting for transfers between devices: 60.5 us -> 0.01 us  [shards(): lax.all_to_all(slots, 'wide', split_axis=0, concat_axis=0, tiled=True)]
    dot_general x14 -> x0, matrix products: 48.4 us -> none  [the longest x4 24.1 us: shards(): jnp.dot(row_part, column_part.T, precision=lax.Precision.HIGHEST, preferr...]
    another operation x6 -> x0, matrix products: 27.5 us -> none  [the longest x4 24.4 us: shards(): jax.scipy.linalg.solve_triangular(factor, raw_column.T, lower=True)]
    unnamed x34 -> x0, local copies, waits for them, and re-layouts: 22.2 us -> none
    reshape x5 -> x0, local copies, waits for them, and re-layouts: 14.2 us -> none  [the longest x2 7.32 us: shards(): middle.reshape(UM, TILE, UM, TILE)]
  transfers between devices with their start and end apart: 6 -> 2, of which waited for: 4 -> 1; matrix products, arithmetic and copies ran while one was open for 32% -> 0% of each run, Pallas kernels for 0% -> 68%
where the time goes in v1:
time: 310 us
  Pallas kernels  239 us (77%)
  waiting for transfers between devices  38.9 us (13%)
  between operations  14.7 us (5%)
  starting transfers between devices  13.1 us (4%)
    pallas_call x1, Pallas kernels, shards(): pl.pallas_call(gather_kernel, out_shape=[shape(8, piece, 8, width), shape...  175 us
    reduce_scatter x1, waiting for transfers between devices, shards(): top_part = lax.psum_scatter(total, 'grp', scatter_dimension=0, tiled=True)  38.9 us
    pallas_call x1, Pallas kernels, shards(): pl.pallas_call(root_kernel, out_shape=[shape(rows_here, width), shape(BLO...  35.4 us
    pallas_call x1, Pallas kernels, shards(): pl.pallas_call(fronts_kernel, out_shape=shape(devices, SLOT, TILE), in_sp...  22 us
    all_to_all x1, starting transfers between devices, shards(): lax.all_to_all(slots, 'wide', split_axis=0, concat_axis=0, tiled=True)  13.1 us
    pallas_call x1, Pallas kernels, shards(): pl.pallas_call(add_kernel, out_shape=shape(BLOCK, BLOCK), in_specs=[smem(...  6.78 us
  transfers between devices with their start and end apart: 2, of which 1 were waited for; matrix products, arithmetic and copies ran while one was open for 0% of the time, Pallas kernels for 68%

profile of v1, /device:TPU:1, one launch (start us, length us, event | category | flops | bytes accessed | tf_op | source)
XLA Modules:
  0.0 309.9 jit_solution(6436180883015121170)
XLA Ops:
  7.8 1.3 reshape_squeeze.7.leaf_map
  9.1 22.0 %fronts.1 = f32[64,136,128]{2,1,0:T(8,128)} custom-call(s32[2]{0:T(128)} %bitcast.24, s32[6]{0:T(128)} %reshape_squeeze.7.leaf_map, s32[1]{0:T(128)} %bitcast.14.mid_tiles, s32[7]{0:T(128)} %bitcast.25, f32[2,512,512]{2,1,0:T(8,128)} %bitcast.19, f32[1024,1024]{1,0:T(8,128)} %bitcast.17), custom_call_target="tpu_custom_call" | custom-call | flops 20000000000 | bytes 11000000 | tf_op jit(solution)/shard_map/fronts/pallas_call | solution.py:429
  31.1 13.1 %all-to-all-start = ((f32[64,136,128]{2,1,0:T(8,128)}), f32[64,136,128]{2,1,0:T(8,128)}, u32[]{:S(2)}, u32[]{:S(2)}) async-start(f32[64,136,128]{2,1,0:T(8,128)} %fronts.1), calls=%async_computation | async-start | bytes 8912896 | tf_op jit(solution)/shard_map/all_to_all | solution.py:449
  44.2 0.0 reduce-scatter.2.cloned.1.call-start
  44.2 175.0 %gather.1 = (f32[8,14,8,512]{3,2,1,0:T(8,128)}, f32[8,14,8,512]{3,2,1,0:T(8,128)}, f32[64,8,512]{2,1,0:T(8,128)}) custom-call(f32[15,8,512]{2,1,0:T(8,128)} %bitcast.15), custom_call_target="tpu_custom_call" | custom-call | tf_op jit(solution)/shard_map/gather/pallas_call | solution.py:401
  219.3 35.4 %root.1 = (f32[120,512]{1,0:T(8,128)}, f32[896,896]{1,0:T(8,128)}) custom-call(s32[1]{0:T(128)} %bitcast.position, f32[512,512]{1,0:T(8,128)} %bitcast.22, f32[896,512]{1,0:T(8,128)} %bitcast.20, f32[896,512]{1,0:T(8,128)} %bitcast.21, f32[120,512]{1,0:T(8,128)} %bitcast.16, f32[896,896]{1,0:T(8,128)} %bitcast.18), custom_call_target="tpu_custom_call" | custom-call | flops 30000001024 | bytes 11000000 | tf_op jit(solution)/shard_map/root/pallas_call | solution.py:450
  254.7 0.0 all-to-all-done.tiles_ref
  254.7 2.7 fusion.spots
  257.4 6.8 %add_tiles.1 = f32[896,896]{1,0:T(8,128)} custom-call(s32[64]{0:T(128)} %fusion.spots, f32[896,896]{1,0:T(8,128)} %get-tuple-element.11.base_ref, f32[64,136,128]{2,1,0:T(8,128)} %all-to-all-done.tiles_ref), custom_call_target="tpu_custom_call" | custom-call | tf_op jit(solution)/shard_map/add_tiles/pallas_call | solution.py:465
  264.1 0.0 reduce-scatter.2.cloned.1.call-update
  264.2 38.9 %reduce-scatter.2.cloned.1.call-done = f32[224,896]{1,0:T(8,128)} async-done(((f32[896,896]{1,0:T(8,128)}), f32[224,896]{1,0:T(8,128)}) %reduce-scatter.2.cloned.1.call-update) | async-done | bytes 802832 | tf_op jit(solution)/shard_map/reduce_scatter | solution.py:473
Async XLA Ops:
  31.1 223.6 %all-to-all-start = ((f32[64,136,128]{2,1,0:T(8,128)}), f32[64,136,128]{2,1,0:T(8,128)}, u32[]{:S(2)}, u32[]{:S(2)}) async-start(f32[64,136,128]{2,1,0:T(8,128)} %fronts.1), calls=%async_computation | async-start | bytes 8912896 | tf_op jit(solution)/shard_map/all_to_all | solution.py:449
  44.2 258.9 %reduce-scatter.2.cloned.1.call-start = ((), (), s32[]{:S(2)}) async-start(), calls=%async_computation.2 | async-start | bytes 4014080 | tf_op jit(solution)/shard_map/reduce_scatter | solution.py:473
Sparse Core Ops, SparseCore 0:
  264.3 38.6 reduce-scatter.1

commit v2 on v1

--- a/solution.py
+++ b/solution.py
@@ -16,6 +16,8 @@
 BLOCK = UR * TILE
 PIVOT = K * TILE
 SLOT = TILE + 8
+GROUPS = 4
+CHUNK = BLOCK // GROUPS
 MESH = pl.DeviceIdType.MESH
 HIGHEST = lax.Precision.HIGHEST
 NN = ((1,), (0,))
@@ -123,8 +125,19 @@
 
 
 def fronts_kernel(
-    leaf_tiles, leaf_map, mid_tiles, mid_map, leaf_ref, mid_ref, slot_ref, whole_ref, couple_ref
+    leaf_tiles,
+    leaf_map,
+    mid_tiles,
+    mid_map,
+    leaf_ref,
+    mid_ref,
+    after_ref,
+    slot_ref,
+    whole_ref,
+    couple_ref,
 ):
+    del after_ref
+
     whole_ref[...] = mid_ref[...]
     slot_ref[...] = jnp.zeros_like(slot_ref)
     leaves = leaf_ref.shape[0]
@@ -274,8 +287,8 @@
         is_panel = jnp.logical_not(is_pivot)
         home = jnp.minimum(chunk, devices - 1)
         return (
+            (column_ref.at[part, slot], column_first.at[slot], part * 8 + block, is_panel),
             (row_ref.at[part, slot], row_first.at[slot], piece, is_panel),
-            (column_ref.at[part, slot], column_first.at[slot], part * 8 + block, is_panel),
             (pivot_ref.at[home], pivot_first.at[0], home, is_pivot),
         )
 
@@ -296,6 +309,16 @@
         def _():
             remote(panel_ref.at[0], target, first_send.at[0, 0], sem, me).wait_recv()
 
+    barrier = pltpu.get_barrier_semaphore()
+
+    def greet(step, carry):
+        pl.semaphore_signal(
+            barrier, inc=1, device_id=(group, (me + step) % devices), device_id_type=MESH
+        )
+        return carry
+
+    lax.fori_loop(1, devices, greet, 0)
+    pl.semaphore_wait(barrier, devices - 1)
     first()
     for i in range(here):
         for which, (target, sem, device, wanted) in enumerate(routes(i)):
@@ -317,11 +340,6 @@
     arrived(pivot_ref.at[me], pivot_first.at[0], me // here)
     partner = me + 1 - 2 * core
     push(pivot_ref.at[me], pivot_send.at[0], pivot_recv.at[0], partner)
-    for slot in range(there):
-        arrived(row_ref.at[q, slot], row_first.at[slot], (devices + there * me + slot) // here)
-    for step in range(1, 4):
-        push(row_ref.at[q], row_send.at[step], row_recv.at[q // 2], p * 8 + (q + 2 * step) % 8)
-    push(row_ref.at[q], row_send.at[0], row_recv.at[4 + q // 2], partner)
     turned = q * 8 + p
     for slot in range(there):
         arrived(column_ref.at[p, slot], column_first.at[slot], (devices + there * turned + slot) // here)
@@ -333,6 +351,11 @@
     pair = pivot_ref.at[pl.ds(me - core, 2)]
     for step in range(1, 8):
         push(pair, pivot_send.at[step], pivot_recv.at[1 + depth], line * 16 + ((depth + step) % 8) * 2 + core)
+    for slot in range(there):
+        arrived(row_ref.at[q, slot], row_first.at[slot], (devices + there * me + slot) // here)
+    for step in range(1, 4):
+        push(row_ref.at[q], row_send.at[step], row_recv.at[q // 2], p * 8 + (q + 2 * step) % 8)
+    push(row_ref.at[q], row_send.at[0], row_recv.at[4 + q // 2], partner)
     landed(column_ref.at[across], column_send.at[0], column_recv.at[16])
     for step in range(1, 4):
         push(
@@ -367,6 +390,51 @@
             @pl.when(wanted & (device != me))
             def _():
                 remote(panel_ref.at[i], target, first_send.at[which, i], sem, device).wait_send()
+
+
+def scatter_kernel(total_ref, part_ref, send_sem, recv_sem):
+    group = lax.axis_index("grp")
+    me = lax.axis_index("wide")
+    barrier = pltpu.get_barrier_semaphore()
+    for step in range(1, GROUPS):
+        pl.semaphore_signal(
+            barrier, inc=1, device_id=((group + step) % GROUPS, me), device_id_type=MESH
+        )
+    stay = pltpu.make_async_copy(
+        total_ref.at[pl.ds(group * CHUNK, CHUNK)], part_ref.at[group], send_sem.at[0]
+    )
+    stay.start()
+    pl.semaphore_wait(barrier, GROUPS - 1)
+
+    def send(step):
+        x = (group + step) % GROUPS
+        return pltpu.make_async_remote_copy(
+            src_ref=total_ref.at[pl.ds(x * CHUNK, CHUNK)],
+            dst_ref=part_ref.at[group],
+            send_sem=send_sem.at[step],
+            recv_sem=recv_sem.at[group],
+            device_id=(x, me),
+            device_id_type=MESH,
+        )
+
+    for step in range(1, GROUPS):
+        send(step).start()
+    stay.wait()
+    for step in range(1, GROUPS):
+        g = (group + step) % GROUPS
+        pltpu.make_async_remote_copy(
+            src_ref=total_ref.at[pl.ds(0, CHUNK)],
+            dst_ref=part_ref.at[g],
+            send_sem=send_sem.at[0],
+            recv_sem=recv_sem.at[g],
+            device_id=(group, me),
+            device_id_type=MESH,
+        ).wait_recv()
+        send(step).wait_send()
+
+
+def sum_kernel(part_ref, out_ref):
+    out_ref[...] = (part_ref[0] + part_ref[1]) + (part_ref[2] + part_ref[3])
 
 
 def vmem():
@@ -420,7 +488,7 @@
             pltpu.SemaphoreType.DMA((11,)),
             pltpu.SemaphoreType.DMA((13,)),
         ],
-        compiler_params=pltpu.CompilerParams(has_side_effects=True),
+        compiler_params=pltpu.CompilerParams(collective_id=0, has_side_effects=True),
         name="gather",
     )(panel.reshape(chunks, 8, width))
     row_rows = row_rows.reshape(BLOCK, width)
@@ -429,7 +497,7 @@
     slots = pl.pallas_call(
         fronts_kernel,
         out_shape=shape(devices, SLOT, TILE),
-        in_specs=[smem()] * 4 + [vmem()] * 2,
+        in_specs=[smem()] * 4 + [vmem()] * 2 + [pl.BlockSpec(memory_space=pl.ANY)],
         out_specs=vmem(),
         scratch_shapes=[
             pltpu.VMEM(mid_entries.shape[2:], jnp.float32),
@@ -445,6 +513,7 @@
         mid_map[0, 0],
         leaf_entries[0],
         mid_entries[0, 0],
+        pivot,
     )
     received = lax.all_to_all(slots, "wide", split_axis=0, concat_axis=0, tiled=True)
     root_panel, block = pl.pallas_call(
@@ -470,7 +539,23 @@
         compiler_params=pltpu.CompilerParams(vmem_limit_bytes=VMEM_BYTES),
         name="add_tiles",
     )(spots, block, received)
-    top_part = lax.psum_scatter(total, "grp", scatter_dimension=0, tiled=True)
+    parts = pl.pallas_call(
+        scatter_kernel,
+        out_shape=shape(GROUPS, CHUNK, BLOCK),
+        in_specs=[vmem()],
+        out_specs=pl.BlockSpec(memory_space=pl.ANY),
+        scratch_shapes=[pltpu.SemaphoreType.DMA((GROUPS,)), pltpu.SemaphoreType.DMA((GROUPS,))],
+        compiler_params=pltpu.CompilerParams(collective_id=1, has_side_effects=True),
+        name="scatter",
+    )(total)
+    top_part = pl.pallas_call(
+        sum_kernel,
+        out_shape=shape(CHUNK, BLOCK),
+        in_specs=[vmem()],
+        out_specs=vmem(),
+        compiler_params=pltpu.CompilerParams(vmem_limit_bytes=VMEM_BYTES),
+        name="sum_groups",
+    )(parts)
     return (root_panel[None], top_part[None])
 
 

time: 310 us -> 269 us (0.87)
  Pallas kernels: 239 us -> 182 us
  waiting for transfers between devices: 38.9 us -> 65.7 us
  between operations: 14.7 us -> 1.31 us
    pallas_call x1, Pallas kernels: 175 us -> 74.6 us  [shards(): pl.pallas_call(gather_kernel, out_shape=[shape(8, piece, 8, width), shape...]
    all_to_all x1, waiting for transfers between devices: 0.01 us -> 65.7 us  [shards(): lax.all_to_all(slots, 'wide', split_axis=0, concat_axis=0, tiled=True)]
    pallas_call x0 -> x2, Pallas kernels: none -> 43.7 us  [the longest x1 40.7 us: shards(): pl.pallas_call(scatter_kernel, out_shape=shape(GROUPS, CHUNK, BLOCK), in_...]
    reduce_scatter x1 -> x0, waiting for transfers between devices: 38.9 us -> none  [shards(): top_part = lax.psum_scatter(total, 'grp', scatter_dimension=0, tiled=True)]
  transfers between devices with their start and end apart: 2 -> 1, of which waited for: 1 -> 1; matrix products, arithmetic and copies ran while one was open for 0% -> 0% of each run, Pallas kernels for 68% -> 13%
where the time goes in v2:
time: 269 us
  Pallas kernels  182 us (68%)
  waiting for transfers between devices  65.7 us (24%)
  starting transfers between devices  15.5 us (6%)
  other arithmetic  2.69 us (1%)
    pallas_call x1, Pallas kernels, shards(): pl.pallas_call(gather_kernel, out_shape=[shape(8, piece, 8, width), shape...  74.6 us
    all_to_all x1, waiting for transfers between devices, shards(): lax.all_to_all(slots, 'wide', split_axis=0, concat_axis=0, tiled=True)  65.7 us
    pallas_call x1, Pallas kernels, shards(): pl.pallas_call(scatter_kernel, out_shape=shape(GROUPS, CHUNK, BLOCK), in_...  40.7 us
    pallas_call x1, Pallas kernels, shards(): pl.pallas_call(root_kernel, out_shape=[shape(rows_here, width), shape(BLO...  35.6 us
    pallas_call x1, Pallas kernels, shards(): pl.pallas_call(fronts_kernel, out_shape=shape(devices, SLOT, TILE), in_sp...  21.7 us
    all_to_all x1, starting transfers between devices, shards(): lax.all_to_all(slots, 'wide', split_axis=0, concat_axis=0, tiled=True)  15.5 us
    pallas_call x1, Pallas kernels, shards(): pl.pallas_call(add_kernel, out_shape=shape(BLOCK, BLOCK), in_specs=[smem(...  6.6 us
  transfers between devices with their start and end apart: 1, of which 1 were waited for; matrix products, arithmetic and copies ran while one was open for 0% of the time, Pallas kernels for 13%

profile of v2, /device:TPU:1, one launch (start us, length us, event | category | flops | bytes accessed | tf_op | source)
XLA Modules:
  0.0 268.7 jit_solution(8133295110689167686)
XLA Ops:
  1.3 1.3 reshape_squeeze.7.leaf_map
  2.5 74.6 %gather.1 = (f32[8,14,8,512]{3,2,1,0:T(8,128)}, f32[8,14,8,512]{3,2,1,0:T(8,128)}, f32[64,8,512]{2,1,0:T(8,128)}) custom-call(f32[15,8,512]{2,1,0:T(8,128)} %bitcast.16), custom_call_target="tpu_custom_call" | custom-call | tf_op jit(solution)/shard_map/gather/pallas_call | solution.py:469
  77.2 21.7 %fronts.1 = f32[64,136,128]{2,1,0:T(8,128)} custom-call(s32[2]{0:T(128)} %bitcast.25, s32[6]{0:T(128)} %reshape_squeeze.7.leaf_map, s32[1]{0:T(128)} %bitcast.14.mid_tiles, s32[7]{0:T(128)} %bitcast.26, f32[2,512,512]{2,1,0:T(8,128)} %bitcast.20, f32[1024,1024]{1,0:T(8,128)} %bitcast.18, f32[512,512]{1,0:T(8,128)} %bitcast.23), custom_call_target="tpu_custom_call" | custom-call | flops 20000000000 | bytes 11000000 | tf_op jit(solution)/shard_map/fronts/pallas_call | solution.py:497
  98.9 15.5 %all-to-all-start = ((f32[64,136,128]{2,1,0:T(8,128)}), f32[64,136,128]{2,1,0:T(8,128)}, u32[]{:S(2)}, u32[]{:S(2)}) async-start(f32[64,136,128]{2,1,0:T(8,128)} %fronts.1), calls=%async_computation | async-start | bytes 8912896 | tf_op jit(solution)/shard_map/all_to_all | solution.py:518
  114.4 35.6 %root.1 = (f32[120,512]{1,0:T(8,128)}, f32[896,896]{1,0:T(8,128)}) custom-call(s32[1]{0:T(128)} %bitcast.position, f32[512,512]{1,0:T(8,128)} %bitcast.24, f32[896,512]{1,0:T(8,128)} %bitcast.21, f32[896,512]{1,0:T(8,128)} %bitcast.22, f32[120,512]{1,0:T(8,128)} %bitcast.17, f32[896,896]{1,0:T(8,128)} %bitcast.19), custom_call_target="tpu_custom_call" | custom-call | flops 30000001024 | bytes 11000000 | tf_op jit(solution)/shard_map/root/pallas_call | solution.py:519
  149.9 65.7 %all-to-all-done.tiles_ref = f32[64,136,128]{2,1,0:T(8,128)} async-done(((f32[64,136,128]{2,1,0:T(8,128)}), f32[64,136,128]{2,1,0:T(8,128)}, u32[]{:S(2)}, u32[]{:S(2)}) %all-to-all-start) | async-done | bytes 4456480 | tf_op jit(solution)/shard_map/all_to_all | solution.py:518
  215.7 2.7 %fusion.spots = s32[64]{0:T(128)} fusion(f32[64,136,128]{2,1,0:T(8,128)} %all-to-all-done.tiles_ref), kind=kLoop, calls=%fused_computation.1 | loop fusion | flops 64 | bytes 512 | tf_op jit(solution)/shard_map/convert_element_type | solution.py:533
  218.4 6.6 %add_tiles.1.total_ref = f32[896,896]{1,0:T(8,128)} custom-call(s32[64]{0:T(128)} %fusion.spots, f32[896,896]{1,0:T(8,128)} %get-tuple-element.11.base_ref, f32[64,136,128]{2,1,0:T(8,128)} %all-to-all-done.tiles_ref), custom_call_target="tpu_custom_call" | custom-call | tf_op jit(solution)/shard_map/add_tiles/pallas_call | solution.py:534
  225.0 40.7 %scatter.1.part_ref = f32[4,224,896]{2,1,0:T(8,128)} custom-call(f32[896,896]{1,0:T(8,128)} %add_tiles.1.total_ref), custom_call_target="tpu_custom_call" | custom-call | tf_op jit(solution)/shard_map/scatter/pallas_call | solution.py:542
  265.7 2.9 %sum_groups.1 = f32[224,896]{1,0:T(8,128)} custom-call(f32[4,224,896]{2,1,0:T(8,128)} %scatter.1.part_ref), custom_call_target="tpu_custom_call" | custom-call | tf_op jit(solution)/shard_map/sum_groups/pallas_call | solution.py:551
Async XLA Ops:
  98.9 116.8 %all-to-all-start = ((f32[64,136,128]{2,1,0:T(8,128)}), f32[64,136,128]{2,1,0:T(8,128)}, u32[]{:S(2)}, u32[]{:S(2)}) async-start(f32[64,136,128]{2,1,0:T(8,128)} %fronts.1), calls=%async_computation | async-start | bytes 8912896 | tf_op jit(solution)/shard_map/all_to_all | solution.py:518

commit v3 on v2

--- a/solution.py
+++ b/solution.py
@@ -15,7 +15,6 @@
 UC = 7
 BLOCK = UR * TILE
 PIVOT = K * TILE
-SLOT = TILE + 8
 GROUPS = 4
 CHUNK = BLOCK // GROUPS
 MESH = pl.DeviceIdType.MESH
@@ -160,7 +159,6 @@
     _, inverse = factor_all([whole_ref[:TILE, :TILE]])
     couple_ref[...] = dot_exact(whole_ref[TILE:, :TILE], inverse[0], NT)
     live = mid_tiles[0]
-    column_spots = lax.broadcasted_iota(jnp.int32, (8, TILE), 1)
     for a in range(UM):
         rows = pl.ds(a * TILE, TILE)
         product = dot_split(couple_ref[rows, :], couple_ref[...])
@@ -171,13 +169,8 @@
             @pl.when((a < live) & (b < live))
             def _():
                 target_column = mid_map[b]
-                row_block, column_block = target_row // UR, target_column // UC
-                slot = row_block * 8 + column_block
-                slot_ref[slot, :TILE, :] = update[:, b * TILE : (b + 1) * TILE]
-                spot = (target_row - row_block * UR) * UC + (target_column - column_block * UC)
-                slot_ref[slot, TILE:, :] = jnp.broadcast_to(
-                    (spot + 1).astype(jnp.float32), (8, TILE)
-                )
+                slot = (target_row // UR) * 8 + target_column // UC
+                slot_ref[slot] = update[:, b * TILE : (b + 1) * TILE]
 
 
 def solve_rows(rows, lower, inverse):
@@ -228,13 +221,13 @@
     out_ref[...] = base_ref[...]
 
     def step(s, carry):
-        spot = spots[s] - 1
+        spot = spots[s]
 
         @pl.when(spot >= 0)
         def _():
             rows = pl.ds(pl.multiple_of((spot // UC) * TILE, TILE), TILE)
             columns = pl.ds(pl.multiple_of((spot % UC) * TILE, TILE), TILE)
-            out_ref[rows, columns] += tiles_ref[s, :TILE, :]
+            out_ref[rows, columns] += tiles_ref[s]
 
         return carry
 
@@ -243,9 +236,11 @@
 
 def gather_kernel(
     panel_ref,
+    note_ref,
     row_ref,
     column_ref,
     pivot_ref,
+    notes_ref,
     first_send,
     local_sem,
     row_first,
@@ -257,6 +252,8 @@
     column_recv,
     pivot_send,
     pivot_recv,
+    note_send,
+    note_recv,
 ):
     group = lax.axis_index("grp")
     me = lax.axis_index("wide")
@@ -319,7 +316,10 @@
 
     lax.fori_loop(1, devices, greet, 0)
     pl.semaphore_wait(barrier, devices - 1)
+    note = pltpu.make_async_copy(note_ref, notes_ref.at[me], note_recv.at[0])
+    note.start()
     first()
+    note.wait()
     for i in range(here):
         for which, (target, sem, device, wanted) in enumerate(routes(i)):
 
@@ -337,9 +337,13 @@
     def landed(target, send, recv):
         remote(target, target, send, recv, me).wait_recv()
 
+    def notes(first_device, count):
+        return notes_ref.at[pl.ds(first_device, count)]
+
     arrived(pivot_ref.at[me], pivot_first.at[0], me // here)
     partner = me + 1 - 2 * core
     push(pivot_ref.at[me], pivot_send.at[0], pivot_recv.at[0], partner)
+    push(notes(me, 1), note_send.at[0], note_recv.at[1], partner)
     turned = q * 8 + p
     for slot in range(there):
         arrived(column_ref.at[p, slot], column_first.at[slot], (devices + there * turned + slot) // here)
@@ -348,9 +352,12 @@
     for step in range(1, 4):
         push(column_ref.at[p], column_send.at[step], column_recv.at[p], ((p + 2 * step) % 8) * 8 + q)
     landed(pivot_ref.at[partner], pivot_send.at[0], pivot_recv.at[0])
+    landed(notes(partner, 1), note_send.at[0], note_recv.at[1])
     pair = pivot_ref.at[pl.ds(me - core, 2)]
     for step in range(1, 8):
-        push(pair, pivot_send.at[step], pivot_recv.at[1 + depth], line * 16 + ((depth + step) % 8) * 2 + core)
+        device = line * 16 + ((depth + step) % 8) * 2 + core
+        push(pair, pivot_send.at[step], pivot_recv.at[1 + depth], device)
+        push(notes(me - core, 2), note_send.at[step], note_recv.at[2 + depth], device)
     for slot in range(there):
         arrived(row_ref.at[q, slot], row_first.at[slot], (devices + there * me + slot) // here)
     for step in range(1, 4):
@@ -367,10 +374,14 @@
         push(row_ref.at[source], row_send.at[3 + step], row_recv.at[4 + source // 2], partner)
     for step in range(1, 8):
         source = (depth + 8 - step) % 8
-        landed(pivot_ref.at[pl.ds(line * 16 + source * 2, 2)], pivot_send.at[step], pivot_recv.at[1 + source])
+        device = line * 16 + source * 2
+        landed(pivot_ref.at[pl.ds(device, 2)], pivot_send.at[step], pivot_recv.at[1 + source])
+        landed(notes(device, 2), note_send.at[step], note_recv.at[2 + source])
     mine = pivot_ref.at[pl.ds(line * 16, 16)]
     for step in range(1, 4):
-        push(mine, pivot_send.at[7 + step], pivot_recv.at[9 + line], ((line + step) % 4) * 16 + depth * 2 + core)
+        device = ((line + step) % 4) * 16 + depth * 2 + core
+        push(mine, pivot_send.at[7 + step], pivot_recv.at[9 + line], device)
+        push(notes(line * 16, 16), note_send.at[7 + step], note_recv.at[10 + line], device)
     for step in range(4):
         source = (q + 1 - 2 * core + 2 * step) % 8
         landed(row_ref.at[source], row_send.at[0], row_recv.at[4 + source // 2])
@@ -382,6 +393,7 @@
     for step in range(1, 4):
         source = (line + 4 - step) % 4
         landed(pivot_ref.at[pl.ds(source * 16, 16)], pivot_send.at[7 + step], pivot_recv.at[9 + source])
+        landed(notes(source * 16, 16), note_send.at[7 + step], note_recv.at[10 + source])
     for copy in sends:
         copy.wait_send()
     for i in range(here):
@@ -466,15 +478,18 @@
     width = panel.shape[1]
     chunks = rows_here // 8
     piece = chunks - 1
-    row_rows, column_rows, pivot = pl.pallas_call(
+    note = jnp.concatenate([mid_map[0, 0], mid_tiles[0]]).astype(jnp.float32)
+    note = jnp.broadcast_to(jnp.pad(note, (0, TILE - UM - 1))[None], (8, TILE))
+    row_rows, column_rows, pivot, notes = pl.pallas_call(
         gather_kernel,
         out_shape=[
             shape(8, piece, 8, width),
             shape(8, piece, 8, width),
             shape(devices, 8, width),
+            shape(devices, 8, TILE),
         ],
-        in_specs=[pl.BlockSpec(memory_space=pl.ANY)],
-        out_specs=[vmem()] * 3,
+        in_specs=[pl.BlockSpec(memory_space=pl.ANY)] * 2,
+        out_specs=[vmem()] * 4,
         scratch_shapes=[
             pltpu.SemaphoreType.DMA((3, chunks)),
             pltpu.SemaphoreType.DMA((3, chunks)),
@@ -487,16 +502,18 @@
             pltpu.SemaphoreType.DMA((17,)),
             pltpu.SemaphoreType.DMA((11,)),
             pltpu.SemaphoreType.DMA((13,)),
+            pltpu.SemaphoreType.DMA((11,)),
+            pltpu.SemaphoreType.DMA((14,)),
         ],
         compiler_params=pltpu.CompilerParams(collective_id=0, has_side_effects=True),
         name="gather",
-    )(panel.reshape(chunks, 8, width))
+    )(panel.reshape(chunks, 8, width), note)
     row_rows = row_rows.reshape(BLOCK, width)
     column_rows = column_rows.reshape(BLOCK, width)
     pivot = pivot.reshape(PIVOT, width)
     slots = pl.pallas_call(
         fronts_kernel,
-        out_shape=shape(devices, SLOT, TILE),
+        out_shape=shape(devices, TILE, TILE),
         in_specs=[smem()] * 4 + [vmem()] * 2 + [pl.BlockSpec(memory_space=pl.ANY)],
         out_specs=vmem(),
         scratch_shapes=[
@@ -530,7 +547,17 @@
         cost_estimate=pl.CostEstimate(flops=30_000_000_000, bytes_accessed=11_000_000, transcendentals=0),
         name="root",
     )(position, pivot, row_rows, column_rows, panel, root_update_entries[0, 0])
-    spots = received[:, TILE, 0].astype(jnp.int32)
+    noted = notes[:, 0, : UM + 1].astype(jnp.int32)
+    targets, live = noted[:, :UM], noted[:, UM:]
+    used = jnp.arange(UM, dtype=jnp.int32)[None, :] < live
+
+    def place(block):
+        return jnp.max(jnp.where(used & (targets // UR == block), targets - block * UR, -1), axis=1)
+
+    row_place, column_place = place(position[0] // 8), place(position[0] % 8)
+    spots = jnp.where(
+        (row_place >= 0) & (column_place >= 0), row_place * UC + column_place, -1
+    )
     total = pl.pallas_call(
         add_kernel,
         out_shape=shape(BLOCK, BLOCK),

time: 269 us -> 265 us (0.985)
  waiting for transfers between devices: 65.7 us -> 58.1 us
  Pallas kernels: 182 us -> 187 us
    all_to_all x1, waiting for transfers between devices: 65.7 us -> 58.1 us  [shards(): lax.all_to_all(slots, 'wide', split_axis=0, concat_axis=0, tiled=True)]
    pallas_call x1, Pallas kernels: 74.6 us -> 79.5 us  [shards(): pl.pallas_call(gather_kernel, out_shape=[shape(8, piece, 8, width), shape...]
  transfers between devices with their start and end apart: 1 -> 1, of which waited for: 1 -> 1; matrix products, arithmetic and copies ran while one was open for 0% -> 1% of each run, Pallas kernels for 13% -> 13%
where the time goes in v3:
time: 265 us
  Pallas kernels  187 us (71%)
  waiting for transfers between devices  58.1 us (22%)
  starting transfers between devices  14 us (5%)
    pallas_call x1, Pallas kernels, shards(): pl.pallas_call(gather_kernel, out_shape=[shape(8, piece, 8, width), shape...  79.5 us
    all_to_all x1, waiting for transfers between devices, shards(): lax.all_to_all(slots, 'wide', split_axis=0, concat_axis=0, tiled=True)  58.1 us
    pallas_call x1, Pallas kernels, shards(): pl.pallas_call(scatter_kernel, out_shape=shape(GROUPS, CHUNK, BLOCK), in_...  40.8 us
    pallas_call x1, Pallas kernels, shards(): pl.pallas_call(root_kernel, out_shape=[shape(rows_here, width), shape(BLO...  35.7 us
    pallas_call x1, Pallas kernels, shards(): pl.pallas_call(fronts_kernel, out_shape=shape(devices, TILE, TILE), in_sp...  21.6 us
    all_to_all x1, starting transfers between devices, shards(): lax.all_to_all(slots, 'wide', split_axis=0, concat_axis=0, tiled=True)  14 us
    pallas_call x1, Pallas kernels, shards(): pl.pallas_call(add_kernel, out_shape=shape(BLOCK, BLOCK), in_specs=[smem(...  6.33 us
  transfers between devices with their start and end apart: 1, of which 1 were waited for; matrix products, arithmetic and copies ran while one was open for 1% of the time, Pallas kernels for 13%

profile of v3, /device:TPU:1, one launch (start us, length us, event | category | flops | bytes accessed | tf_op | source)
XLA Modules:
  0.0 264.9 jit_solution(17761340682201943085)
XLA Ops:
  1.3 1.3 reshape_squeeze.7.leaf_map
  2.6 0.7 add_convert_fusion
  3.3 0.6 broadcast_in_dim.20.note_ref
  3.9 79.5 %gather.1 = (f32[8,14,8,512]{3,2,1,0:T(8,128)}, f32[8,14,8,512]{3,2,1,0:T(8,128)}, f32[64,8,512]{2,1,0:T(8,128)}, f32[64,8,128]{2,1,0:T(8,128)}) custom-call(f32[15,8,512]{2,1,0:T(8,128)} %bitcast.20, f32[8,128]{1,0:T(8,128)} %broadcast_in_dim.20.note_ref), custom_call_target="tpu_custom_call" | custom-call | tf_op jit(solution)/shard_map/gather/pallas_call | solution.py:483
  83.4 21.6 %fronts.1 = f32[64,128,128]{2,1,0:T(8,128)} custom-call(s32[2]{0:T(128)} %bitcast.31, s32[6]{0:T(128)} %reshape_squeeze.7.leaf_map, s32[1]{0:T(128)} %bitcast.16.mid_tiles, s32[7]{0:T(128)} %bitcast.30, f32[2,512,512]{2,1,0:T(8,128)} %bitcast.24, f32[1024,1024]{1,0:T(8,128)} %bitcast.22, f32[512,512]{1,0:T(8,128)} %bitcast.27), custom_call_target="tpu_custom_call" | custom-call | flops 20000000000 | bytes 11000000 | tf_op jit(solution)/shard_map/fronts/pallas_call | solution.py:514
  105.1 14.0 %all-to-all-start = ((f32[64,128,128]{2,1,0:T(8,128)}), f32[64,128,128]{2,1,0:T(8,128)}, u32[]{:S(2)}, u32[]{:S(2)}) async-start(f32[64,128,128]{2,1,0:T(8,128)} %fronts.1), calls=%async_computation | async-start | bytes 8388608 | tf_op jit(solution)/shard_map/all_to_all | solution.py:535
  119.1 1.0 slice_convert_fusion
  120.1 0.2 slice_reduce_fusion
  120.2 0.2 select_reduce_fusion.1
  120.4 0.5 and_select_fusion.spots
  121.0 35.7 %root.1 = (f32[120,512]{1,0:T(8,128)}, f32[896,896]{1,0:T(8,128)}) custom-call(s32[1]{0:T(128)} %bitcast.position, f32[512,512]{1,0:T(8,128)} %bitcast.28, f32[896,512]{1,0:T(8,128)} %bitcast.25, f32[896,512]{1,0:T(8,128)} %bitcast.26, f32[120,512]{1,0:T(8,128)} %bitcast.21, f32[896,896]{1,0:T(8,128)} %bitcast.23), custom_call_target="tpu_custom_call" | custom-call | flops 30000001024 | bytes 11000000 | tf_op jit(solution)/shard_map/root/pallas_call | solution.py:536
  156.7 58.1 %all-to-all-done.tiles_ref = f32[64,128,128]{2,1,0:T(8,128)} async-done(((f32[64,128,128]{2,1,0:T(8,128)}), f32[64,128,128]{2,1,0:T(8,128)}, u32[]{:S(2)}, u32[]{:S(2)}) %all-to-all-start) | async-done | bytes 4194336 | tf_op jit(solution)/shard_map/all_to_all | solution.py:535
  214.7 6.3 %add_tiles.1.total_ref = f32[896,896]{1,0:T(8,128)} custom-call(s32[64]{0:T(128)} %and_select_fusion.spots, f32[896,896]{1,0:T(8,128)} %get-tuple-element.13.base_ref, f32[64,128,128]{2,1,0:T(8,128)} %all-to-all-done.tiles_ref), custom_call_target="tpu_custom_call" | custom-call | tf_op jit(solution)/shard_map/add_tiles/pallas_call | solution.py:561
  221.1 40.8 %scatter.1.part_ref = f32[4,224,896]{2,1,0:T(8,128)} custom-call(f32[896,896]{1,0:T(8,128)} %add_tiles.1.total_ref), custom_call_target="tpu_custom_call" | custom-call | tf_op jit(solution)/shard_map/scatter/pallas_call | solution.py:569
  261.9 2.9 %sum_groups.1 = f32[224,896]{1,0:T(8,128)} custom-call(f32[4,224,896]{2,1,0:T(8,128)} %scatter.1.part_ref), custom_call_target="tpu_custom_call" | custom-call | tf_op jit(solution)/shard_map/sum_groups/pallas_call | solution.py:578
  (1 shorter events, 0.0 us)
Async XLA Ops:
  105.1 109.7 %all-to-all-start = ((f32[64,128,128]{2,1,0:T(8,128)}), f32[64,128,128]{2,1,0:T(8,128)}, u32[]{:S(2)}, u32[]{:S(2)}) async-start(f32[64,128,128]{2,1,0:T(8,128)} %fronts.1), calls=%async_computation | async-start | bytes 8388608 | tf_op jit(solution)/shard_map/all_to_all | solution.py:535
